TPU v7x, 32 devices: a whole 2x2x4 slice. The times are simulated.
32 devices in a mesh: row: 4 (over y, x), col: 8 (over z, core).
Axes of the slice: x: 2, y: 2, z: 4, core: 2. Of those that a mesh axis runs over, the one named last changes fastest.
Arguments:
- operator: float32 [4096, 4096], P('row', 'col'), may hold values from -0.09375 to 0.09375
- state: float32 [4096, 4096], P('row', 'col'), may hold values from -60 to 60, as said below
- source: float32 [4096, 4096], P('row', 'col'), may hold values from -60 to 60, as said below
Outputs:
- state_next: float32 [4096, 4096], P('row', 'col')
- operator_fourth: float32 [4096, 4096], P('row', 'col')
Inputs may be any that keep to these rules, and one draw needn't show every extreme that they name: symmetric: state equals its transpose. symmetric: source equals its transpose.
All inputs are finite; a program needn't handle non-finite values.
Results may differ from a plain program's by a relative error of at most 0.000098.
Values sent between devices are 32-bit elements; how exact they have to be, the bound alone decides.
No kernel may reach another device: no remote copies, remote signals or barrier semaphores. Data moves between devices by JAX's collectives and lax.ppermute only.
A program may use at most 128 MiB of HBM per device.

v0:
```python
import jax
import jax.numpy as jnp
from jax import lax
from jax.sharding import PartitionSpec as P


def matmul(left, right):
    return jnp.dot(left, right, preferred_element_type=jnp.float32, precision=lax.Precision.HIGHEST)


def split_pieces(block, groups):
    rows, columns = block.shape
    width = columns // groups
    pieces = block.reshape(2, columns, groups, width).transpose(2, 0, 3, 1)
    return pieces.reshape(2 * groups, width, columns)


def join_pieces(pieces, groups):
    count, width, columns = pieces.shape
    joined = pieces.reshape(groups, 2, width, columns).transpose(1, 0, 2, 3)
    return joined.reshape(2 * groups * width, columns)


def folder(panel, piece):
    return matmul(panel, piece)


def on_device(operator, state, source):
    groups = lax.axis_size("row")
    row_panel = lax.all_gather(operator, "col", axis=1, tiled=True)
    product = matmul(row_panel, lax.all_gather(state, "row", axis=0, tiled=True))
    square = matmul(row_panel, lax.all_gather(operator, "row", axis=0, tiled=True))
    moved = lax.all_to_all(
        lax.all_to_all(
            split_pieces(product, groups), "row", split_axis=0, concat_axis=0, tiled=True
        ),
        "col",
        split_axis=0,
        concat_axis=0,
        tiled=True,
    )
    turned = join_pieces(
        lax.all_to_all(moved, "row", split_axis=0, concat_axis=0, tiled=True), groups
    )
    state_next = folder(row_panel, lax.all_gather(turned, "row", axis=0, tiled=True)) + source
    square_panel = lax.all_gather(square, "col", axis=1, tiled=True)
    operator_fourth = folder(square_panel, lax.all_gather(square, "row", axis=0, tiled=True))
    return (state_next, operator_fourth)


def solution(mesh):
    in_specs = (P("row", "col"), P("row", "col"), P("row", "col"))
    out_specs = (P("row", "col"), P("row", "col"))
    return jax.shard_map(
        on_device, mesh=mesh, in_specs=in_specs, out_specs=out_specs, check_vma=False
    )
```

profile of v0, /device:TPU:0, one launch (start us, length us, event | category | flops | bytes accessed | tf_op | source)
XLA Modules:
  0.0 784.8 jit_solution(5429908569219231628)
XLA Ops:
  7.2 0.0 all-gather.9.cloned.1.call-start
  7.2 0.7 all-gather.9.cloned.1.call-update
  7.9 0.0 all-gather.7.cloned.1.call-start
  7.9 0.7 all-gather.7.cloned.1.call-update
  8.6 0.0 all-gather.13.cloned.1.call-start
  8.7 0.7 all-gather.13.cloned.1.call-update
  9.4 0.0 all-gather.11.cloned.1.call-start
  9.4 90.6 %all-gather.9.cloned.1.call-done = f32[4096,512]{1,0:T(8,128)} async-done(((f32[1024,512]{1,0:T(8,128)}), f32[4096,512]{1,0:T(8,128)}) %all-gather.9.cloned.1.call-update) | async-done | bytes 8388624 | tf_op jit(solution)/shard_map/all_gather | solution.py:31
  100.1 152.7 %all-gather.7.cloned.1.call-done = f32[1024,4096]{1,0:T(8,128)} async-done(((f32[1024,512]{1,0:T(8,128)}), f32[1024,4096]{1,0:T(8,128)}) %all-gather.7.cloned.1.call-update) | async-done | bytes 16777232 | tf_op jit(solution)/shard_map/all_gather | solution.py:30
  252.8 31.0 %fusion = f32[1024,512]{1,0:T(8,128)} fusion(f32[1024,4096]{1,0:T(8,128)} %all-gather.7.cloned.1.call-done, f32[4096,512]{1,0:T(8,128)} %all-gather.9.cloned.1.call-done), kind=kOutput, calls=%fused_computation.1 | convolution fusion | flops 25769803776 | bytes 27262976 | tf_op jit(solution)/shard_map/dot_general | solution.py:8
  283.7 1.9 reshape.16
  285.7 1.8 copy.7
  287.5 51.3 %all_to_all.15 = f32[8,128,512]{2,1,0:T(8,128)S(1)} all-to-all(f32[8,128,512]{2,1,0:T(8,128)} %bitcast.18), channel_id=1, replica_groups=mesh['row'=4,'col'=8] {'row'}, dimensions={0} | all-to-all | bytes 4194304 | tf_op jit(solution)/shard_map/all_to_all | solution.py:34
  338.8 51.5 %all_to_all.16 = f32[8,128,512]{2,1,0:T(8,128)S(1)} all-to-all(f32[8,128,512]{2,1,0:T(8,128)S(1)} %all_to_all.15), channel_id=1, replica_groups=mesh['row'=4,'col'=8] {'col'}, dimensions={0} | all-to-all | bytes 4194304 | tf_op jit(solution)/shard_map/all_to_all | solution.py:33
  390.3 27.7 %all_to_all.17 = f32[8,128,512]{2,1,0:T(8,128)S(1)} all-to-all(f32[8,128,512]{2,1,0:T(8,128)S(1)} %all_to_all.16), channel_id=1, replica_groups=mesh['row'=4,'col'=8] {'row'}, dimensions={0} | all-to-all | bytes 4194304 | tf_op jit(solution)/shard_map/all_to_all | solution.py:43
  418.0 1.6 copy.8
  419.6 0.0 all-gather.11.cloned.1.call-update
  419.6 0.0 copy-start
  419.6 0.2 all-gather.17.cloned.1.call-start
  419.9 0.0 all-gather.13.cloned.1.call-done
  419.9 31.1 %fusion.1 = f32[1024,512]{1,0:T(8,128)} fusion(f32[1024,4096]{1,0:T(8,128)} %all-gather.7.cloned.1.call-done, f32[4096,512]{1,0:T(8,128)} %all-gather.13.cloned.1.call-done), kind=kOutput, calls=%fused_computation.2 | convolution fusion | flops 25769803776 | bytes 27262976 | tf_op jit(solution)/shard_map/dot_general | solution.py:8
  451.0 0.0 all-gather.17.cloned.1.call-update
  451.0 0.0 all-gather.15.cloned.1.call-start
  451.0 0.5 all-gather.15.cloned.1.call-update
  451.6 0.0 copy-done
  451.6 1.8 copy.9
  453.4 51.8 %all-gather.11.cloned.1.call-done = f32[4096,512]{1,0:T(8,128)} async-done(((f32[1024,512]{1,0:T(8,128)}), f32[4096,512]{1,0:T(8,128)}) %all-gather.11.cloned.1.call-update) | async-done | bytes 8388624 | tf_op jit(solution)/shard_map/all_gather | solution.py:45
  505.2 56.7 %bitcast_add_fusion = f32[1024,512]{0,1:T(8,128)S(1)} fusion(f32[1024,512]{0,1:T(8,128)} %copy.9, f32[4096,512]{1,0:T(8,128)} %all-gather.11.cloned.1.call-done, f32[1024,4096]{1,0:T(8,128)} %all-gather.7.cloned.1.call-done), kind=kOutput, calls=%fused_computation | convolution fusion | flops 25770328064 | bytes 29360128 | tf_op jit(solution)/shard_map/dot_general | solution.py:8
  562.0 1.8 copy.10
  563.8 30.6 %all-gather.17.cloned.1.call-done = f32[4096,512]{1,0:T(8,128)} async-done(((f32[1024,512]{1,0:T(8,128)}), f32[4096,512]{1,0:T(8,128)}) %all-gather.17.cloned.1.call-update) | async-done | bytes 8388624 | tf_op jit(solution)/shard_map/all_gather | solution.py:47
  594.4 152.6 %all-gather.15.cloned.1.call-done = f32[1024,4096]{1,0:T(8,128)} async-done(((f32[1024,512]{1,0:T(8,128)}), f32[1024,4096]{1,0:T(8,128)}) %all-gather.15.cloned.1.call-update) | async-done | bytes 16777232 | tf_op jit(solution)/shard_map/all_gather | solution.py:46
  747.0 31.0 %fusion.2 = f32[1024,512]{1,0:T(8,128)} fusion(f32[1024,4096]{1,0:T(8,128)} %all-gather.15.cloned.1.call-done, f32[4096,512]{1,0:T(8,128)} %all-gather.17.cloned.1.call-done), kind=kOutput, calls=%fused_computation.3 | convolution fusion | flops 25769803776 | bytes 27262976 | tf_op jit(solution)/shard_map/dot_general | solution.py:8
Async XLA Ops:
  7.2 92.9 %all-gather.9.cloned.1.call-start = ((), (), s32[]{:S(2)}) async-start(), calls=%async_computation.4 | async-start | bytes 10485760 | tf_op jit(solution)/shard_map/all_gather | solution.py:31
  7.9 244.9 %all-gather.7.cloned.1.call-start = ((), (), s32[]{:S(2)}) async-start(), calls=%async_computation.3 | async-start | bytes 18874368 | tf_op jit(solution)/shard_map/all_gather | solution.py:30
  8.6 411.2 %all-gather.13.cloned.1.call-start = ((), (), s32[]{:S(2)}) async-start(), calls=%async_computation.6 | async-start | bytes 10485760 | tf_op jit(solution)/shard_map/all_gather | solution.py:32
  9.4 495.9 %all-gather.11.cloned.1.call-start = ((), (), s32[]{:S(2)}) async-start(), calls=%async_computation.5 | async-start | bytes 10485760 | tf_op jit(solution)/shard_map/all_gather | solution.py:45
  419.6 32.0 %copy-start = (f32[1024,512]{1,0:T(8,128)S(1)}, f32[1024,512]{1,0:T(8,128)}, u32[]{:S(2)}) copy-start(f32[1024,512]{1,0:T(8,128)} %param.5) | copy-start | bytes 6291460
  419.6 174.8 %all-gather.17.cloned.1.call-start = ((), (), s32[]{:S(2)}) async-start(), calls=%async_computation.8 | async-start | bytes 10485760 | tf_op jit(solution)/shard_map/all_gather | solution.py:47
  451.0 296.0 %all-gather.15.cloned.1.call-start = ((), (), s32[]{:S(2)}) async-start(), calls=%async_computation.7 | async-start | bytes 18874368 | tf_op jit(solution)/shard_map/all_gather | solution.py:46
Sparse Core Ops, SparseCore 0:
  9.8 90.1 all-gather.8
  101.7 151.0 all-gather.6
  254.6 107.1 all-gather.12
  419.7 85.4 all-gather.10
  506.9 87.4 all-gather.16
  595.9 151.0 all-gather.14
where the time goes:
time: 785 us
  waiting for transfers between devices  481 us (61%)
  matrix products  150 us (19%)
  blocking collectives  131 us (17%)
  between operations  14.2 us (2%)
  local copies, waits for them, and re-layouts  8.94 us (1%)
    all_gather x1, waiting for transfers between devices, on_device(): row_panel = lax.all_gather(operator, 'col', axis=1, tiled=True)  153 us
    all_gather x1, waiting for transfers between devices, on_device(): square_panel = lax.all_gather(square, 'col', axis=1, tiled=True)  153 us
    dot_general x4, matrix products, matmul(): jnp.dot(left, right, preferred_element_type=jnp.float32, precision=lax.Pr...  150 us
    all_gather x1, waiting for transfers between devices, on_device(): lax.all_gather(state, 'row', axis=0, tiled=True)  90.6 us
    all_gather x1, waiting for transfers between devices, on_device(): lax.all_gather(turned, 'row', axis=0, tiled=True)  51.8 us
    all_to_all x1, blocking collectives, on_device(): lax.all_to_all(lax.all_to_all(split_pieces(product, groups), 'row', split...  51.5 us
    all_to_all x1, blocking collectives, on_device(): lax.all_to_all(split_pieces(product, groups), 'row', split_axis=0, concat...  51.3 us
    all_gather x1, waiting for transfers between devices, on_device(): lax.all_gather(square, 'row', axis=0, tiled=True)  30.6 us
  transfers between devices with their start and end apart: 6, of which 5 were waited for; matrix products, arithmetic and copies ran while one was open for 16% of the time, Pallas kernels for 0%

commit v1 on v0

--- a/solution.py
+++ b/solution.py
@@ -2,6 +2,17 @@
 import jax.numpy as jnp
 from jax import lax
 from jax.sharding import PartitionSpec as P
+
+
+def turned_line(array, axis, d):
+    n_dev = lax.axis_size(axis)
+    route = [(i, (i + 1) % n_dev) for i in range(n_dev)]
+    parts = [array]
+    for far in range(1, n_dev):
+        parts = [lax.ppermute(parts[0], axis, route), *parts]
+    whole = jnp.concatenate(parts, axis=d)
+    turn = (lax.axis_index(axis) + 1) * parts[-1].shape[d]
+    return jnp.roll(whole, turn, axis=d)
 
 
 def matmul(left, right):
@@ -27,7 +38,7 @@
 
 def on_device(operator, state, source):
     groups = lax.axis_size("row")
-    row_panel = lax.all_gather(operator, "col", axis=1, tiled=True)
+    row_panel = turned_line(operator, "col", 1)
     product = matmul(row_panel, lax.all_gather(state, "row", axis=0, tiled=True))
     square = matmul(row_panel, lax.all_gather(operator, "row", axis=0, tiled=True))
     moved = lax.all_to_all(

time: 785 us -> 743 us (0.946)
  local copies, waits for them, and re-layouts: 8.94 us -> 47.9 us
  blocking collectives: 131 us -> 98.9 us
  matrix products: 150 us -> 124 us
  waiting for transfers between devices: 481 us -> 457 us
    ppermute x0 -> x7, waiting for transfers between devices: none -> 192 us  [turned_line(): parts = [lax.ppermute(parts[0], axis, route), *parts]]
    all_gather x1 -> x0, waiting for transfers between devices: 153 us -> none  [on_device(): row_panel = lax.all_gather(operator, 'col', axis=1, tiled=True)]
    all_gather x1, waiting for transfers between devices: 90.6 us -> 0.01 us  [on_device(): lax.all_gather(state, 'row', axis=0, tiled=True)]
    unnamed x4 -> x35, local copies, waits for them, and re-layouts: 3.63 us -> 41.1 us
    all_to_all x1, blocking collectives: 51.3 us -> 19.7 us  [on_device(): lax.all_to_all(split_pieces(product, groups), 'row', split_axis=0, concat...]
    all_gather x1, waiting for transfers between devices: 30.6 us -> 58 us  [on_device(): lax.all_gather(square, 'row', axis=0, tiled=True)]
    dot_general x4, matrix products: 150 us -> 124 us  [matmul(): jnp.dot(left, right, preferred_element_type=jnp.float32, precision=lax.Pr...]
  transfers between devices with their start and end apart: 6 -> 12, of which waited for: 5 -> 10; matrix products, arithmetic and copies ran while one was open for 16% -> 18% of each run, Pallas kernels for 0% -> 0%
where the time goes in v1:
time: 743 us
  waiting for transfers between devices  457 us (62%)
  matrix products  124 us (17%)
  blocking collectives  98.9 us (13%)
  local copies, waits for them, and re-layouts  47.9 us (6%)
  between operations  13.9 us (2%)
    ppermute x7, waiting for transfers between devices, turned_line(): parts = [lax.ppermute(parts[0], axis, route), *parts]  192 us
    all_gather x1, waiting for transfers between devices, on_device(): square_panel = lax.all_gather(square, 'col', axis=1, tiled=True)  153 us
    dot_general x4, matrix products, matmul(): jnp.dot(left, right, preferred_element_type=jnp.float32, precision=lax.Pr...  124 us
    all_gather x1, waiting for transfers between devices, on_device(): lax.all_gather(square, 'row', axis=0, tiled=True)  58 us
    all_gather x1, waiting for transfers between devices, on_device(): lax.all_gather(turned, 'row', axis=0, tiled=True)  53.6 us
    all_to_all x1, blocking collectives, on_device(): lax.all_to_all(lax.all_to_all(split_pieces(product, groups), 'row', split...  51.5 us
    unnamed x35, local copies, waits for them, and re-layouts  41.1 us
    all_to_all x1, blocking collectives, on_device(): lax.all_to_all(moved, 'row', split_axis=0, concat_axis=0, tiled=True)  27.7 us
  transfers between devices with their start and end apart: 12, of which 10 were waited for; matrix products, arithmetic and copies ran while one was open for 18% of the time, Pallas kernels for 0%

profile of v1, /device:TPU:0, one launch (start us, length us, event | category | flops | bytes accessed | tf_op | source)
XLA Modules:
  0.0 742.7 jit_solution(6406625914624660397)
XLA Ops:
  8.0 27.9 %collective-permute-done = f32[1024,512]{1,0:T(8,128)} collective-permute-done((f32[1024,512]{1,0:T(8,128)}, f32[1024,512]{1,0:T(8,128)}, u32[]{:S(2)}, u32[]{:S(2)}) %collective-permute-start) | collective-permute-done | bytes 2097184 | tf_op jit(solution)/shard_map/ppermute | solution.py:12
  35.8 27.5 %collective-permute-done.1 = f32[1024,512]{1,0:T(8,128)S(1)} collective-permute-done((f32[1024,512]{1,0:T(8,128)}, f32[1024,512]{1,0:T(8,128)S(1)}, u32[]{:S(2)}, u32[]{:S(2)}) %collective-permute-start.1) | collective-permute-done | bytes 2097184 | tf_op jit(solution)/shard_map/ppermute | solution.py:12
  64.7 27.3 %collective-permute-done.2 = f32[1024,512]{1,0:T(8,128)S(1)} collective-permute-done((f32[1024,512]{1,0:T(8,128)S(1)}, f32[1024,512]{1,0:T(8,128)S(1)}, u32[]{:S(2)}, u32[]{:S(2)}) %collective-permute-start.2) | collective-permute-done | bytes 2097184 | tf_op jit(solution)/shard_map/ppermute | solution.py:12
  93.3 27.3 %collective-permute-done.3 = f32[1024,512]{1,0:T(8,128)S(1)} collective-permute-done((f32[1024,512]{1,0:T(8,128)S(1)}, f32[1024,512]{1,0:T(8,128)S(1)}, u32[]{:S(2)}, u32[]{:S(2)}) %collective-permute-start.3) | collective-permute-done | bytes 2097184 | tf_op jit(solution)/shard_map/ppermute | solution.py:12
  121.9 27.3 %collective-permute-done.4 = f32[1024,512]{1,0:T(8,128)S(1)} collective-permute-done((f32[1024,512]{1,0:T(8,128)S(1)}, f32[1024,512]{1,0:T(8,128)S(1)}, u32[]{:S(2)}, u32[]{:S(2)}) %collective-permute-start.4) | collective-permute-done | bytes 2097184 | tf_op jit(solution)/shard_map/ppermute | solution.py:12
  150.4 27.4 %collective-permute-done.5 = f32[1024,512]{1,0:T(8,128)} collective-permute-done((f32[1024,512]{1,0:T(8,128)S(1)}, f32[1024,512]{1,0:T(8,128)}, u32[]{:S(2)}, u32[]{:S(2)}) %collective-permute-start.5) | collective-permute-done | bytes 2097184 | tf_op jit(solution)/shard_map/ppermute | solution.py:12
  177.9 27.5 %collective-permute-done.6 = f32[1024,512]{1,0:T(8,128)} collective-permute-done((f32[1024,512]{1,0:T(8,128)}, f32[1024,512]{1,0:T(8,128)}, u32[]{:S(2)}, u32[]{:S(2)}) %collective-permute-start.6) | collective-permute-done | bytes 2097184 | tf_op jit(solution)/shard_map/ppermute | solution.py:12
  205.4 3.1 constant_dynamic-update-slice_fusion.15
  208.4 3.1 constant_dynamic-update-slice_fusion.14
  211.5 3.2 constant_dynamic-update-slice_fusion.13
  214.7 3.2 constant_dynamic-update-slice_fusion.12
  219.4 1.6 constant_dynamic-update-slice_fusion.10
  221.0 3.6 constant_dynamic-update-slice_fusion.9
  224.6 1.5 constant_dynamic-update-slice_fusion.8
  226.1 3.1 constant_dynamic-update-slice_fusion.7
  229.1 3.0 constant_dynamic-update-slice_fusion.6
  232.2 1.5 constant_dynamic-update-slice_fusion.5
  238.1 3.1 constant_dynamic-update-slice_fusion.1
  241.1 1.5 constant_dynamic-update-slice_fusion
  242.7 31.0 %fusion.4 = f32[1024,512]{1,0:T(8,128)} fusion(f32[4096,512]{1,0:T(8,128)} %all-gather.6.cloned.1.call-done, f32[1024,8192]{1,0:T(8,128)} %constant_dynamic-update-slice_fusion, s32[]{:T(128)S(6)} %select_n.14), kind=kOutput, calls=%fused_computation.4 | convolution fusion | flops 25769803776 | bytes 27262980 | tf_op jit(solution)/shard_map/dot_general | solution.py:19
  273.6 1.9 reshape.16
  275.6 1.8 copy.5
  277.4 19.7 %all_to_all.15 = f32[8,128,512]{2,1,0:T(8,128)S(1)} all-to-all(f32[8,128,512]{2,1,0:T(8,128)} %bitcast.13), channel_id=1, replica_groups=mesh['row'=4,'col'=8] {'row'}, dimensions={0} | all-to-all | bytes 4194304 | tf_op jit(solution)/shard_map/all_to_all | solution.py:45
  297.0 51.5 %all_to_all.16 = f32[8,128,512]{2,1,0:T(8,128)S(1)} all-to-all(f32[8,128,512]{2,1,0:T(8,128)S(1)} %all_to_all.15), channel_id=1, replica_groups=mesh['row'=4,'col'=8] {'col'}, dimensions={0} | all-to-all | bytes 4194304 | tf_op jit(solution)/shard_map/all_to_all | solution.py:44
  348.5 27.7 %all_to_all.17 = f32[8,128,512]{2,1,0:T(8,128)S(1)} all-to-all(f32[8,128,512]{2,1,0:T(8,128)S(1)} %all_to_all.16), channel_id=1, replica_groups=mesh['row'=4,'col'=8] {'row'}, dimensions={0} | all-to-all | bytes 4194304 | tf_op jit(solution)/shard_map/all_to_all | solution.py:54
  376.3 1.5 copy.6
  378.0 31.2 %fusion = f32[1024,512]{1,0:T(8,128)} fusion(f32[4096,512]{1,0:T(8,128)} %all-gather.10.cloned.1.call-done, f32[1024,8192]{1,0:T(8,128)} %constant_dynamic-update-slice_fusion, s32[]{:T(128)S(6)} %select_n.14), kind=kOutput, calls=%fused_computation | convolution fusion | flops 25769803776 | bytes 27262980 | tf_op jit(solution)/shard_map/dot_general | solution.py:19
  409.8 53.6 %all-gather.8.cloned.1.call-done = f32[4096,512]{1,0:T(8,128)} async-done(((f32[1024,512]{1,0:T(8,128)}), f32[4096,512]{1,0:T(8,128)}) %all-gather.8.cloned.1.call-update) | async-done | bytes 8388624 | tf_op jit(solution)/shard_map/all_gather | solution.py:56
  463.4 31.2 %fusion.6 = f32[1024,512]{1,0:T(8,128)} fusion(f32[1024,512]{1,0:T(8,128)S(1)} %copy-done.9, f32[4096,512]{1,0:T(8,128)} %all-gather.8.cloned.1.call-done, f32[1024,8192]{1,0:T(8,128)} %constant_dynamic-update-slice_fusion, s32[]{:T(128)S(6)} %select_n.14), kind=kOutput, calls=%fused_computation.6 | convolution fusion | flops 25770328064 | bytes 29360132 | tf_op jit(solution)/shard_map/dot_general | solution.py:19
  494.6 58.0 %all-gather.14.cloned.1.call-done = f32[4096,512]{1,0:T(8,128)} async-done(((f32[1024,512]{1,0:T(8,128)}), f32[4096,512]{1,0:T(8,128)}) %all-gather.14.cloned.1.call-update) | async-done | bytes 8388624 | tf_op jit(solution)/shard_map/all_gather | solution.py:58
  552.6 152.6 %all-gather.12.cloned.1.call-done = f32[1024,4096]{1,0:T(8,128)} async-done(((f32[1024,512]{1,0:T(8,128)}), f32[1024,4096]{1,0:T(8,128)}) %all-gather.12.cloned.1.call-update) | async-done | bytes 16777232 | tf_op jit(solution)/shard_map/all_gather | solution.py:57
  705.2 31.0 %fusion.12 = f32[1024,512]{1,0:T(8,128)} fusion(f32[1024,4096]{1,0:T(8,128)} %all-gather.12.cloned.1.call-done, f32[4096,512]{1,0:T(8,128)} %all-gather.14.cloned.1.call-done), kind=kOutput, calls=%fused_computation.26 | convolution fusion | flops 25769803776 | bytes 27262976 | tf_op jit(solution)/shard_map/dot_general | solution.py:19
  (43 shorter events, 12.9 us)
Async XLA Ops:
  7.2 217.4 %copy-start = (f32[1024,512]{1,0:T(8,128)S(1)}, f32[1024,512]{1,0:T(8,128)}, u32[]{:S(2)}) copy-start(f32[1024,512]{1,0:T(8,128)} %param.3) | copy-start | bytes 6291460
  7.2 235.5 %all-gather.6.cloned.1.call-start = ((), (), s32[]{:S(2)}) async-start(), calls=%async_computation.3 | async-start | bytes 10485760 | tf_op jit(solution)/shard_map/all_gather | solution.py:42
  7.2 28.6 %collective-permute-start = (f32[1024,512]{1,0:T(8,128)}, f32[1024,512]{1,0:T(8,128)}, u32[]{:S(2)}, u32[]{:S(2)}) collective-permute-start(f32[1024,512]{1,0:T(8,128)} %param.3), channel_id=1, source_target_pairs={{0,1},{1,2},{2,3},{3,4},{4,5},{5,6},{6,7},{7,0},{8,9},{9,10},{10,1... | collective-permute-start | bytes 6291464 | tf_op jit(solution)/shard_map/ppermute | solution.py:12
  7.9 370.1 %all-gather.10.cloned.1.call-start = ((), (), s32[]{:S(2)}) async-start(), calls=%async_computation.5 | async-start | bytes 10485760 | tf_op jit(solution)/shard_map/all_gather | solution.py:43
  35.8 27.5 %collective-permute-start.1 = (f32[1024,512]{1,0:T(8,128)}, f32[1024,512]{1,0:T(8,128)S(1)}, u32[]{:S(2)}, u32[]{:S(2)}) collective-permute-start(f32[1024,512]{1,0:T(8,128)} %collective-permute-done), channel_id=1, source_target_pairs={{0,1},{1,2},{2,3},{3,4},{4,5},{5,6},{6,7},{7,0},{8,9},{9,10},{10,1... | collective-permute-start | bytes 6291464 | tf_op jit(solution)/shard_map/ppermute | solution.py:12
  63.3 1.4 copy-start.1
  64.7 27.3 %collective-permute-start.2 = (f32[1024,512]{1,0:T(8,128)S(1)}, f32[1024,512]{1,0:T(8,128)S(1)}, u32[]{:S(2)}, u32[]{:S(2)}) collective-permute-start(f32[1024,512]{1,0:T(8,128)S(1)} %collective-permute-done.1), channel_id=1, source_target_pairs={{0,1},{1,2},{2,3},{3,4},{4,5},{5,6},{6,7},{7,0},{8,9},{9,10},{10,1... | collective-permute-start | bytes 6291464 | tf_op jit(solution)/shard_map/ppermute | solution.py:12
  91.9 1.4 copy-start.3
  93.3 27.3 %collective-permute-start.3 = (f32[1024,512]{1,0:T(8,128)S(1)}, f32[1024,512]{1,0:T(8,128)S(1)}, u32[]{:S(2)}, u32[]{:S(2)}) collective-permute-start(f32[1024,512]{1,0:T(8,128)S(1)} %collective-permute-done.2), channel_id=1, source_target_pairs={{0,1},{1,2},{2,3},{3,4},{4,5},{5,6},{6,7},{7,0},{8,9},{9,10},{10,1... | collective-permute-start | bytes 6291464 | tf_op jit(solution)/shard_map/ppermute | solution.py:12
  120.5 1.3 copy-start.5
  121.9 27.3 %collective-permute-start.4 = (f32[1024,512]{1,0:T(8,128)S(1)}, f32[1024,512]{1,0:T(8,128)S(1)}, u32[]{:S(2)}, u32[]{:S(2)}) collective-permute-start(f32[1024,512]{1,0:T(8,128)S(1)} %collective-permute-done.3), channel_id=1, source_target_pairs={{0,1},{1,2},{2,3},{3,4},{4,5},{5,6},{6,7},{7,0},{8,9},{9,10},{10,1... | collective-permute-start | bytes 6291464 | tf_op jit(solution)/shard_map/ppermute | solution.py:12
  149.1 1.3 copy-start.7
  150.4 27.4 %collective-permute-start.5 = (f32[1024,512]{1,0:T(8,128)S(1)}, f32[1024,512]{1,0:T(8,128)}, u32[]{:S(2)}, u32[]{:S(2)}) collective-permute-start(f32[1024,512]{1,0:T(8,128)S(1)} %collective-permute-done.4), channel_id=1, source_target_pairs={{0,1},{1,2},{2,3},{3,4},{4,5},{5,6},{6,7},{7,0},{8,9},{9,10},{10,1... | collective-permute-start | bytes 6291464 | tf_op jit(solution)/shard_map/ppermute | solution.py:12
  177.8 27.6 %collective-permute-start.6 = (f32[1024,512]{1,0:T(8,128)}, f32[1024,512]{1,0:T(8,128)}, u32[]{:S(2)}, u32[]{:S(2)}) collective-permute-start(f32[1024,512]{1,0:T(8,128)} %collective-permute-done.5), channel_id=1, source_target_pairs={{0,1},{1,2},{2,3},{3,4},{4,5},{5,6},{6,7},{7,0},{8,9},{9,10},{10,1... | collective-permute-start | bytes 6291464 | tf_op jit(solution)/shard_map/ppermute | solution.py:12
  177.8 285.6 %all-gather.8.cloned.1.call-start = ((), (), s32[]{:S(2)}) async-start(), calls=%async_computation.4 | async-start | bytes 10485760 | tf_op jit(solution)/shard_map/all_gather | solution.py:56
  177.9 40.1 %copy-start.4 = (f32[1024,512]{1,0:T(8,128)S(1)}, f32[1024,512]{1,0:T(8,128)}, u32[]{:S(2)}) copy-start(f32[1024,512]{1,0:T(8,128)} %copy-done.3) | copy-start | bytes 6291460
  177.9 41.5 %copy-start.2 = (f32[1024,512]{1,0:T(8,128)S(1)}, f32[1024,512]{1,0:T(8,128)}, u32[]{:S(2)}) copy-start(f32[1024,512]{1,0:T(8,128)} %copy-done.1) | copy-start | bytes 6291460
  211.5 20.6 %copy-start.8 = (f32[1024,512]{1,0:T(8,128)S(1)}, f32[1024,512]{1,0:T(8,128)}, u32[]{:S(2)}) copy-start(f32[1024,512]{1,0:T(8,128)} %copy-done.7) | copy-start | bytes 6291460
  214.7 18.9 %copy-start.6 = (f32[1024,512]{1,0:T(8,128)S(1)}, f32[1024,512]{1,0:T(8,128)}, u32[]{:S(2)}) copy-start(f32[1024,512]{1,0:T(8,128)} %copy-done.5) | copy-start | bytes 6291460
  377.8 85.6 %copy-start.9 = (f32[1024,512]{1,0:T(8,128)S(1)}, f32[1024,512]{1,0:T(8,128)}, u32[]{:S(2)}) copy-start(f32[1024,512]{1,0:T(8,128)} %param.5) | copy-start | bytes 6291460
  377.8 174.8 %all-gather.14.cloned.1.call-start = ((), (), s32[]{:S(2)}) async-start(), calls=%async_computation.7 | async-start | bytes 10485760 | tf_op jit(solution)/shard_map/all_gather | solution.py:58
  409.2 295.9 %all-gather.12.cloned.1.call-start = ((), (), s32[]{:S(2)}) async-start(), calls=%async_computation.6 | async-start | bytes 18874368 | tf_op jit(solution)/shard_map/all_gather | solution.py:57
Sparse Core Ops, SparseCore 0:
  9.8 90.1 all-gather.5
  177.9 89.1 all-gather.9
  377.9 85.4 all-gather.7
  465.1 87.4 all-gather.13
  554.1 151.0 all-gather.11
